TPU v7x, 256 devices: a whole 4x4x8 slice. The times are simulated.
256 devices in a mesh: leaf: 16 (over y, x), blk: 16 (over z, core).
Axes of the slice: x: 4, y: 4, z: 8, core: 2. Of those that a mesh axis runs over, the one named last changes fastest.
Arguments:
- leaf_rhs: bfloat16 [81920, 256], P(('leaf', 'blk')), may hold values from -6 to 6
- leaf_inverse: bfloat16 [81920, 5120], P(('leaf', 'blk')), may hold values from -0.078125 to 0.078125
- leaf_lower: bfloat16 [32768, 5120], P(('leaf', 'blk')), may hold values from -0.078125 to 0.078125
- sep_rhs: bfloat16 [4, 16384, 256], P(None, ('leaf', 'blk')), may hold values from -6 to 6
- sep_inverse: bfloat16 [16384, 30720], P(('leaf', 'blk'))
- sep_lower: bfloat16 [32768, 14336], P(('leaf', 'blk'))
- slot_map: int32 [4, 256, 2], P(None, ('leaf', 'blk')), may hold values from 0 to 5, as said below
Outputs:
- leaf_solution: bfloat16 [81920, 256], P(('leaf', 'blk'))
- sep_solution: bfloat16 [4, 16384, 256], P(None, ('leaf', 'blk'))
Inputs may be any that keep to these rules, and one draw needn't show every extreme that they name: For every level below the top, slot_map[h-1, q] holds two different numbers of 0 to 5; at the top level it holds 0 and 1 in some order.
All inputs are finite; a program needn't handle non-finite values.
Results may differ from a plain program's by a relative error of at most 0.015.
Values may be sent and summed in bfloat16 or wider, within the bound.
A program may use at most 128 MiB of HBM per device.

v0:
```python
import jax
import jax.numpy as jnp
from jax import lax
from jax.sharding import PartitionSpec as P


def partner(value, axis, apart):
    mask = 2**apart
    pairs = [(source, source ^ mask) for source in range(lax.axis_size(axis))]
    return lax.ppermute(value, axis, pairs)


def from_everyone(shard, axis):
    length = lax.axis_size(axis)
    return lax.all_to_all(
        jnp.broadcast_to(shard[None], (length, *shard.shape)), axis, 0, 0, tiled=True
    )


def laid_out(blocks, dim):
    blocks = jnp.moveaxis(blocks, 0, dim)
    shape = blocks.shape
    return blocks.reshape(*shape[:dim], shape[dim] * shape[dim + 1], *shape[dim + 2 :])


def gather_directly(shard, axis, dim):
    blocks = from_everyone(shard, axis)
    return laid_out(blocks, dim)


def pair_merge(mine, partner_rows, bit_index):
    upper_bit = jnp.bitwise_and(jnp.right_shift(lax.axis_index("leaf"), bit_index), 1)
    lower_half = jnp.where(upper_bit == 1, partner_rows, mine)
    upper_half = jnp.where(upper_bit == 1, mine, partner_rows)
    return jnp.concatenate([lower_half, upper_half], axis=0)


def group_rows(pieces, height):
    joined = pieces
    for bit_index in range(height):
        partner_rows = partner(joined, "leaf", bit_index)
        joined = pair_merge(joined, partner_rows, bit_index)
    spread = lax.all_gather(joined, "blk", axis=0, tiled=True)
    spread = spread.reshape(lax.axis_size("blk"), 2**height, pieces.shape[0], pieces.shape[1])
    return jnp.transpose(spread, (1, 0, 2, 3)).reshape(-1, pieces.shape[1])


def on_device(leaf_rhs, leaf_inverse, leaf_lower, sep_rhs, sep_inverse, sep_lower, slot_map):
    columns = leaf_rhs.shape[1]
    levels = sep_rhs.shape[0]
    pivots = sep_rhs.shape[1]
    base_width = pivots * lax.axis_size("blk")
    section = leaf_inverse
    leaf_solution = jnp.dot(
        section, gather_directly(leaf_rhs, "blk", 0), preferred_element_type=jnp.float32
    ).astype(jnp.bfloat16)
    section = leaf_lower
    update = -jnp.dot(
        section, gather_directly(leaf_solution, "blk", 0), preferred_element_type=jnp.float32
    )
    solutions = []
    for height in range(1, levels + 1):
        at_root = height == levels
        front_slots = 1 if at_root else 3
        slot_rows = update.reshape(2, pivots, columns)
        onehot = (
            slot_map[height - 1, 0][:, None]
            == jnp.arange(2 * front_slots, dtype=jnp.int32)[None, :]
        ).astype(jnp.float32)
        mixed = jnp.einsum("st,spr->tpr", onehot, slot_rows, precision=lax.Precision.HIGHEST)
        received = partner(mixed[front_slots:].astype(jnp.bfloat16), "leaf", height - 1).astype(
            jnp.float32
        )
        front_rows = mixed[:front_slots] + received
        pivot_front = (sep_rhs[height - 1].astype(jnp.float32) + front_rows[0]).astype(jnp.bfloat16)
        width_now = base_width * 2**height
        offset = base_width * (2**height - 2)
        gathered = group_rows(pivot_front, height)
        solved = jnp.dot(
            sep_inverse[:, offset : offset + width_now],
            gathered,
            preferred_element_type=jnp.float32,
        ).astype(jnp.bfloat16)
        solutions.append(solved)
        if not at_root:
            spread = group_rows(solved, height)
            product = jnp.dot(
                sep_lower[:, offset : offset + width_now],
                spread,
                preferred_element_type=jnp.float32,
            )
            update = front_rows[1:].reshape(2 * pivots, columns) - product
    return (leaf_solution, jnp.stack(solutions))


def solution(mesh):
    return jax.shard_map(
        on_device,
        mesh=mesh,
        in_specs=(
            P(("leaf", "blk"), None),
            P(("leaf", "blk"), None),
            P(("leaf", "blk"), None),
            P(None, ("leaf", "blk"), None),
            P(("leaf", "blk"), None),
            P(("leaf", "blk"), None),
            P(None, ("leaf", "blk"), None),
        ),
        out_specs=(P(("leaf", "blk"), None), P(None, ("leaf", "blk"), None)),
        check_vma=False,
    )
```

profile of v0, /device:TPU:1, one launch (start us, length us, event | category | flops | bytes accessed | tf_op | source)
XLA Modules:
  0.0 590.2 jit_solution(4690270651904076409)
XLA Ops:
  8.5 71.9 %all_to_all.10 = bf16[16,320,256]{2,1,0:T(8,128)(2,1)S(1)} all-to-all(bf16[16,320,256]{2,1,0:T(8,128)(2,1)S(1)} %broadcast_in_dim.4), channel_id=1, replica_groups=mesh['leaf'=16,'blk'=16] {'blk'}, dimensions={0} | all-to-all | bytes 5242880 | tf_op jit(solution)/shard_map/all_to_all | solution.py:15
  81.5 1.7 broadcast_in_dim.5
  83.2 3.8 all-to-all-start.1
  87.2 58.6 %all-to-all-done.1 = bf16[16,320,256]{2,1,0:T(8,128)(2,1)S(1)} async-done(((bf16[16,320,256]{2,1,0:T(8,128)(2,1)}), bf16[16,320,256]{2,1,0:T(8,128)(2,1)S(1)}, u32[]{:S(2)}, u32[]{:S(2)}) %all-to-all-start.1) | async-done | bytes 2621472 | tf_op jit(solution)/shard_map/all_to_all | solution.py:15
  145.9 1.8 convolution_negate_fusion
  149.6 2.6 collective-permute-done
  153.7 1.6 collective-permute-done.1
  156.0 41.3 %all-gather.8.cloned.1.call-done = bf16[2048,256]{1,0:T(8,128)(2,1)} async-done(((bf16[128,256]{1,0:T(8,128)(2,1)}), bf16[2048,256]{1,0:T(8,128)(2,1)}) %all-gather.8.cloned.1.call-update) | async-done | bytes 1048592 | tf_op jit(solution)/shard_map/all_gather | solution.py:43
  201.1 1.6 collective-permute-done.2
  203.5 38.2 %all-gather.10.cloned.1.call-done = bf16[2048,256]{1,0:T(8,128)(2,1)} async-done(((bf16[128,256]{1,0:T(8,128)(2,1)}), bf16[2048,256]{1,0:T(8,128)(2,1)}) %all-gather.10.cloned.1.call-update) | async-done | bytes 1048592 | tf_op jit(solution)/shard_map/all_gather | solution.py:43
  245.1 2.8 collective-permute-start.3
  247.9 2.8 collective-permute-done.3
  252.1 1.6 collective-permute-done.4
  253.7 2.8 collective-permute-start.5
  256.5 1.9 collective-permute-done.5
  259.2 41.3 %all-gather.12.cloned.1.call-done = bf16[4096,256]{1,0:T(8,128)(2,1)} async-done(((bf16[256,256]{1,0:T(8,128)(2,1)}), bf16[4096,256]{1,0:T(8,128)(2,1)}) %all-gather.12.cloned.1.call-update) | async-done | bytes 2097168 | tf_op jit(solution)/shard_map/all_gather | solution.py:43
  300.4 1.8 copy.28
  302.3 1.5 convolution_convert_fusion.3
  305.0 1.6 collective-permute-done.6
  306.7 2.8 collective-permute-start.7
  309.4 1.9 collective-permute-done.7
  312.1 40.2 %all-gather.14.cloned.1.call-done = bf16[4096,256]{1,0:T(8,128)(2,1)} async-done(((bf16[256,256]{1,0:T(8,128)(2,1)}), bf16[4096,256]{1,0:T(8,128)(2,1)}) %all-gather.14.cloned.1.call-update) | async-done | bytes 2097168 | tf_op jit(solution)/shard_map/all_gather | solution.py:43
  352.3 1.8 copy.29
  354.2 1.7 bitcast_subtract_fusion.1
  357.8 2.8 collective-permute-done.8
  362.2 1.6 collective-permute-done.9
  363.8 2.8 collective-permute-start.10
  366.6 1.9 collective-permute-done.10
  369.8 2.6 collective-permute-done.11
  373.3 44.7 %all-gather.16.cloned.1.call-done = bf16[8192,256]{1,0:T(8,128)(2,1)} async-done(((bf16[512,256]{1,0:T(8,128)(2,1)}), bf16[8192,256]{1,0:T(8,128)(2,1)}) %all-gather.16.cloned.1.call-update) | async-done | bytes 4194320 | tf_op jit(solution)/shard_map/all_gather | solution.py:43
  418.0 2.5 copy.33
  420.5 2.0 convolution_convert_fusion.1
  423.9 1.6 collective-permute-done.12
  425.5 2.8 collective-permute-start.13
  428.2 1.9 collective-permute-done.13
  431.5 2.6 collective-permute-done.14
  435.0 44.0 %all-gather.18.cloned.1.call-done = bf16[8192,256]{1,0:T(8,128)(2,1)} async-done(((bf16[512,256]{1,0:T(8,128)(2,1)}), bf16[8192,256]{1,0:T(8,128)(2,1)}) %all-gather.18.cloned.1.call-update) | async-done | bytes 4194320 | tf_op jit(solution)/shard_map/all_gather | solution.py:43
  479.0 2.7 copy.34
  483.5 2.8 collective-permute-start.15
  489.1 1.6 collective-permute-done.16
  490.8 2.8 collective-permute-start.17
  493.5 1.9 collective-permute-done.17
  496.8 2.6 collective-permute-done.18
  499.5 2.8 collective-permute-start.19
  502.3 5.4 collective-permute-done.19
  508.7 60.0 %all-gather.20.cloned.1.call-done = bf16[16384,256]{1,0:T(8,128)(2,1)} async-done(((bf16[1024,256]{1,0:T(8,128)(2,1)}), bf16[16384,256]{1,0:T(8,128)(2,1)}) %all-gather.20.cloned.1.call-update) | async-done | bytes 8388624 | tf_op jit(solution)/shard_map/all_gather | solution.py:43
  568.7 8.4 %copy.38 = bf16[16,16,64,256]{3,2,0,1:T(8,128)(2,1)} copy(bf16[16,16,64,256]{3,2,1,0:T(8,128)(2,1)} %bitcast.105) | data formatting | bytes 16777216 | tf_op jit(solution)/shard_map/reshape | solution.py:44
  577.1 5.6 fusion.10
  (114 shorter events, 35.6 us)
Async XLA Ops:
  7.2 73.2 %copy-start = (bf16[320,5120]{1,0:T(8,128)(2,1)S(1)}, bf16[320,5120]{1,0:T(8,128)(2,1)}, u32[]{:S(2)}) copy-start(bf16[320,5120]{1,0:T(8,128)(2,1)} %param.8) | copy-start | bytes 9830404
  81.4 1.7 copy-start.5
  83.2 3.8 copy-start.7
  83.2 62.7 %all-to-all-start.1 = ((bf16[16,320,256]{2,1,0:T(8,128)(2,1)}), bf16[16,320,256]{2,1,0:T(8,128)(2,1)S(1)}, u32[]{:S(2)}, u32[]{:S(2)}) async-start(bf16[16,320,256]{2,1,0:T(8,128)(2,1)} %broadcast_in_dim.5), calls=%async_computation.1 | async-start | bytes 5242880 | tf_op jit(solution)/shard_map/all_to_all | solution.py:15
  87.0 65.3 %slice-start.2 = ((bf16[4,64,256]{2,1,0:T(8,128)(2,1)}), bf16[1,64,256]{2,1,0:T(8,128)(2,1)S(1)}, s32[]{:S(2)}) async-start(bf16[4,64,256]{2,1,0:T(8,128)(2,1)} %param.10), calls=%async_computation.11 | async-start | bytes 65536 | tf_op jit(solution)/shard_map/slice | solution.py:75
  87.0 110.3 %all-gather.8.cloned.1.call-start = ((), (), s32[]{:S(2)}) async-start(), calls=%async_computation.2 | async-start | bytes 1114112 | tf_op jit(solution)/shard_map/all_gather | solution.py:43
  148.3 3.9 collective-permute-start
  152.4 2.9 collective-permute-start.1
  155.9 85.8 %all-gather.10.cloned.1.call-start = ((), (), s32[]{:S(2)}) async-start(), calls=%async_computation.3 | async-start | bytes 1114112 | tf_op jit(solution)/shard_map/all_gather | solution.py:43
  199.8 2.9 collective-permute-start.2
  203.4 97.1 %all-gather.12.cloned.1.call-start = ((), (), s32[]{:S(2)}) async-start(), calls=%async_computation.4 | async-start | bytes 2228224 | tf_op jit(solution)/shard_map/all_gather | solution.py:43
  203.5 47.3 %copy-start.6 = (bf16[4,64,256]{2,1,0:T(8,128)(2,1)S(1)}, bf16[4,64,256]{2,1,0:T(8,128)(2,1)}, u32[]{:S(2)}) copy-start(bf16[4,64,256]{2,1,0:T(8,128)(2,1)} %param.10) | copy-start | bytes 393220
  245.1 5.7 collective-permute-start.3
  250.8 61.3 %copy-start.4 = (f32[3,64,256]{2,1,0:T(8,128)}, f32[3,64,256]{2,1,0:T(8,128)S(1)}, u32[]{:S(2)}) copy-start(f32[3,64,256]{2,1,0:T(8,128)S(1)} %copy_add_fusion.1) | copy-start | bytes 589828
  250.8 2.9 collective-permute-start.4
  253.7 4.7 collective-permute-start.5
  259.1 93.2 %all-gather.14.cloned.1.call-start = ((), (), s32[]{:S(2)}) async-start(), calls=%async_computation.5 | async-start | bytes 2228224 | tf_op jit(solution)/shard_map/all_gather | solution.py:43
  303.8 2.9 collective-permute-start.6
  306.7 4.7 collective-permute-start.7
  312.1 106.0 %all-gather.16.cloned.1.call-start = ((), (), s32[]{:S(2)}) async-start(), calls=%async_computation.6 | async-start | bytes 4456448 | tf_op jit(solution)/shard_map/all_gather | solution.py:43
  312.1 42.0 %slice-start.1 = ((f32[3,64,256]{2,1,0:T(8,128)}), f32[2,64,256]{2,1,0:T(8,128)S(1)}, s32[]{:S(2)}) async-start(f32[3,64,256]{2,1,0:T(8,128)} %copy-done.4), calls=%async_computation.10 | async-start | bytes 262144 | tf_op jit(solution)/shard_map/slice | solution.py:92
  356.5 4.2 collective-permute-start.8
  360.7 74.3 %copy-start.3 = (f32[3,64,256]{2,1,0:T(8,128)}, f32[3,64,256]{2,1,0:T(8,128)S(1)}, u32[]{:S(2)}) copy-start(f32[3,64,256]{2,1,0:T(8,128)S(1)} %copy_add_fusion) | copy-start | bytes 589828
  360.7 3.0 collective-permute-start.9
  363.8 4.7 collective-permute-start.10
  368.5 3.9 collective-permute-start.11
  373.3 105.7 %all-gather.18.cloned.1.call-start = ((), (), s32[]{:S(2)}) async-start(), calls=%async_computation.7 | async-start | bytes 4456448 | tf_op jit(solution)/shard_map/all_gather | solution.py:43
  422.6 2.9 collective-permute-start.12
  425.5 4.7 collective-permute-start.13
  430.2 3.9 collective-permute-start.14
  434.9 133.8 %all-gather.20.cloned.1.call-start = ((), (), s32[]{:S(2)}) async-start(), calls=%async_computation.8 | async-start | bytes 8912896 | tf_op jit(solution)/shard_map/all_gather | solution.py:43
  479.0 3.3 copy-start.2
  479.0 3.3 slice-start
  483.5 4.4 collective-permute-start.15
  487.9 2.9 collective-permute-start.16
  490.8 4.7 collective-permute-start.17
  495.5 3.9 collective-permute-start.18
  499.5 8.2 %collective-permute-start.19 = (bf16[512,256]{1,0:T(8,128)(2,1)S(1)}, bf16[512,256]{1,0:T(8,128)(2,1)S(1)}, u32[]{:S(2)}, u32[]{:S(2)}) collective-permute-start(bf16[512,256]{1,0:T(8,128)(2,1)S(1)} %pad_maximum_fusion.3), channel_id=1, source_target_pairs={{0,128},{16,144},{32,160},{48,176},{64,192},{80,208},{96,224},{112... | collective-permute-start | bytes 786440 | tf_op jit(solution)/shard_map/ppermute | solution.py:10
  577.1 6.3 %copy-start.1 = (bf16[320,5120]{1,0:T(8,128)(2,1)S(1)}, bf16[320,5120]{1,0:T(8,128)(2,1)}, u32[]{:S(2)}) copy-start(bf16[320,5120]{1,0:T(8,128)(2,1)} %param.8) | copy-start | bytes 9830404
Sparse Core Ops, SparseCore 0:
  156.0 41.1 all-gather.7
  203.5 38.2 all-gather.9
  259.2 41.1 all-gather.11
  312.2 40.1 all-gather.13
  373.4 44.6 all-gather.15
  435.0 43.8 all-gather.17
  508.8 59.8 all-gather.19
where the time goes:
time: 591 us; the launch traced here: 590 us
  waiting for transfers between devices  412 us (70%)
  blocking collectives  71.9 us (12%)
  starting transfers between devices  42 us (7%)
  local copies, waits for them, and re-layouts  24.3 us (4%)
  matrix products  19 us (3%)
  between operations  14.7 us (2%)
  other arithmetic  6.32 us (1%)
    all_gather x7, waiting for transfers between devices, group_rows(): spread = lax.all_gather(joined, 'blk', axis=0, tiled=True)  310 us
    all_to_all x1, blocking collectives, from_everyone(): lax.all_to_all(jnp.broadcast_to(shard[None], (length, *shard.shape)), axi...  71.9 us
    all_to_all x1, waiting for transfers between devices, from_everyone(): lax.all_to_all(jnp.broadcast_to(shard[None], (length, *shard.shape)), axi...  58.6 us
    ppermute x20, waiting for transfers between devices, partner(): return lax.ppermute(value, axis, pairs)  43.5 us
    ppermute x20, starting transfers between devices, partner(): return lax.ppermute(value, axis, pairs)  38 us
    reshape x7, local copies, waits for them, and re-layouts, group_rows(): spread.reshape(lax.axis_size('blk'), 2 ** height, pieces.shape[0], pieces...  19.8 us
  transfers between devices with their start and end apart: 28, of which 28 were waited for; matrix products, arithmetic and copies ran while one was open for 0% of the time, Pallas kernels for 0%

commit v1 on v0

--- a/solution.py
+++ b/solution.py
@@ -2,6 +2,13 @@
 import jax.numpy as jnp
 from jax import lax
 from jax.sharding import PartitionSpec as P
+
+
+def _update_teams(axis_key, inputs):
+    part_now = lax.axis_size(axis_key)
+    plain = jnp.stack([inputs] * part_now, axis=0)
+    work_now = lax.all_to_all(plain, axis_key, 0, 0)
+    return jnp.concatenate(work_now, axis=0)
 
 
 def partner(value, axis, apart):
@@ -40,7 +47,7 @@
     for bit_index in range(height):
         partner_rows = partner(joined, "leaf", bit_index)
         joined = pair_merge(joined, partner_rows, bit_index)
-    spread = lax.all_gather(joined, "blk", axis=0, tiled=True)
+    spread = _update_teams("blk", joined)
     spread = spread.reshape(lax.axis_size("blk"), 2**height, pieces.shape[0], pieces.shape[1])
     return jnp.transpose(spread, (1, 0, 2, 3)).reshape(-1, pieces.shape[1])
 

time: 591 us -> 843 us (1.43)
  blocking collectives: 71.9 us -> 467 us
  waiting for transfers between devices: 412 us -> 273 us
  starting transfers between devices: 42 us -> 57.5 us
  between operations: 14.7 us -> 1.25 us
    all_to_all x0 -> x4, blocking collectives: none -> 395 us  [_update_teams(): work_now = lax.all_to_all(plain, axis_key, 0, 0)]
    all_gather x7 -> x0, waiting for transfers between devices: 310 us -> none  [group_rows(): spread = lax.all_gather(joined, 'blk', axis=0, tiled=True)]
    all_to_all x0 -> x3, waiting for transfers between devices: none -> 170 us  [_update_teams(): work_now = lax.all_to_all(plain, axis_key, 0, 0)]
    reshape x7 -> x0, local copies, waits for them, and re-layouts: 19.8 us -> none  [group_rows(): spread.reshape(lax.axis_size('blk'), 2 ** height, pieces.shape[0], pieces...]
    all_to_all x0 -> x3, starting transfers between devices: none -> 14.8 us  [_update_teams(): work_now = lax.all_to_all(plain, axis_key, 0, 0)]
    transpose x0 -> x7, local copies, waits for them, and re-layouts: none -> 12 us  [group_rows(): return jnp.transpose(spread, (1, 0, 2, 3)).reshape(-1, pieces.shape[1])]
  transfers between devices with their start and end apart: 28 -> 24, of which waited for: 28 -> 24; matrix products, arithmetic and copies ran while one was open for 0% -> 0% of each run, Pallas kernels for 0% -> 0%
where the time goes in v1:
time: 843 us
  blocking collectives  467 us (55%)
  waiting for transfers between devices  273 us (32%)
  starting transfers between devices  57.5 us (7%)
  local copies, waits for them, and re-layouts  23.1 us (3%)
  matrix products  19 us (2%)
    all_to_all x4, blocking collectives, _update_teams(): work_now = lax.all_to_all(plain, axis_key, 0, 0)  395 us
    all_to_all x3, waiting for transfers between devices, _update_teams(): work_now = lax.all_to_all(plain, axis_key, 0, 0)  170 us
    all_to_all x1, blocking collectives, from_everyone(): lax.all_to_all(jnp.broadcast_to(shard[None], (length, *shard.shape)), axi...  71.9 us
    all_to_all x1, waiting for transfers between devices, from_everyone(): lax.all_to_all(jnp.broadcast_to(shard[None], (length, *shard.shape)), axi...  58.7 us
    ppermute x20, waiting for transfers between devices, partner(): return lax.ppermute(value, axis, pairs)  43.6 us
    ppermute x20, starting transfers between devices, partner(): return lax.ppermute(value, axis, pairs)  39.1 us
  transfers between devices with their start and end apart: 24, of which 24 were waited for; matrix products, arithmetic and copies ran while one was open for 0% of the time, Pallas kernels for 0%

profile of v1, /device:TPU:1, one launch (start us, length us, event | category | flops | bytes accessed | tf_op | source)
XLA Modules:
  0.0 842.5 jit_solution(5193098779468351939)
XLA Ops:
  2.0 71.9 %all_to_all.45 = bf16[16,320,256]{2,1,0:T(8,128)(2,1)S(1)} all-to-all(bf16[16,320,256]{2,1,0:T(8,128)(2,1)S(1)} %broadcast_in_dim.4), channel_id=1, replica_groups=mesh['leaf'=16,'blk'=16] {'blk'}, dimensions={0} | all-to-all | bytes 5242880 | tf_op jit(solution)/shard_map/all_to_all | solution.py:22
  74.9 1.7 broadcast_in_dim.5
  76.7 3.6 all-to-all-start.1
  80.6 58.7 %all-to-all-done.1 = bf16[16,320,256]{2,1,0:T(8,128)(2,1)S(1)} async-done(((bf16[16,320,256]{2,1,0:T(8,128)(2,1)}), bf16[16,320,256]{2,1,0:T(8,128)(2,1)S(1)}, u32[]{:S(2)}, u32[]{:S(2)}) %all-to-all-start.1) | async-done | bytes 2621472 | tf_op jit(solution)/shard_map/all_to_all | solution.py:22
  139.2 1.8 convolution_negate_fusion
  143.0 2.6 collective-permute-done
  147.0 1.6 collective-permute-done.1
  148.7 36.7 %all_to_all.46 = bf16[16,128,256]{2,1,0:T(8,128)(2,1)S(1)} all-to-all(bf16[16,128,256]{2,1,0:T(8,128)(2,1)S(1)} %stack.24), channel_id=1, replica_groups=mesh['leaf'=16,'blk'=16] {'blk'}, dimensions={0} | all-to-all | bytes 2097152 | tf_op jit(solution)/shard_map/all_to_all | solution.py:10
  188.0 1.6 collective-permute-done.2
  190.7 4.1 all-to-all-start.3
  195.0 27.9 %all-to-all-done.3 = bf16[16,128,256]{2,1,0:T(8,128)(2,1)S(1)} async-done(((bf16[16,128,256]{2,1,0:T(8,128)(2,1)}), bf16[16,128,256]{2,1,0:T(8,128)(2,1)S(1)}, u32[]{:S(2)}, u32[]{:S(2)}) %all-to-all-start.3) | async-done | bytes 1048608 | tf_op jit(solution)/shard_map/all_to_all | solution.py:10
  225.0 2.8 collective-permute-start.3
  227.8 2.3 collective-permute-done.3
  231.5 2.0 collective-permute-done.4
  233.5 2.8 collective-permute-start.5
  236.4 1.9 collective-permute-done.5
  238.5 57.2 %all_to_all.47 = bf16[16,256,256]{2,1,0:T(8,128)(2,1)S(1)} all-to-all(bf16[16,256,256]{2,1,0:T(8,128)(2,1)S(1)} %stack.27), channel_id=1, replica_groups=mesh['leaf'=16,'blk'=16] {'blk'}, dimensions={0} | all-to-all | bytes 4194304 | tf_op jit(solution)/shard_map/all_to_all | solution.py:10
  298.7 1.6 collective-permute-done.6
  300.3 2.8 collective-permute-start.7
  303.1 2.4 collective-permute-done.7
  307.1 4.7 all-to-all-start.5
  311.9 49.0 %all-to-all-done.5 = bf16[16,256,256]{2,1,0:T(8,128)(2,1)S(1)} async-done(((bf16[16,256,256]{2,1,0:T(8,128)(2,1)}), bf16[16,256,256]{2,1,0:T(8,128)(2,1)S(1)}, u32[]{:S(2)}, u32[]{:S(2)}) %all-to-all-start.5) | async-done | bytes 2097184 | tf_op jit(solution)/shard_map/all_to_all | solution.py:10
  361.0 1.7 bitcast_subtract_fusion.1
  363.4 1.6 collective-permute-start.8
  365.0 2.7 collective-permute-done.8
  370.7 2.8 collective-permute-start.10
  373.5 1.9 collective-permute-done.10
  376.8 2.5 collective-permute-done.11
  379.8 104.7 %all_to_all.48 = bf16[16,512,256]{2,1,0:T(8,128)(2,1)S(1)} all-to-all(bf16[16,512,256]{2,1,0:T(8,128)(2,1)S(1)} %stack.30), channel_id=1, replica_groups=mesh['leaf'=16,'blk'=16] {'blk'}, dimensions={0} | all-to-all | bytes 8388608 | tf_op jit(solution)/shard_map/all_to_all | solution.py:10
  485.1 2.0 convolution_convert_fusion.1
  488.4 1.6 collective-permute-done.12
  490.0 2.8 collective-permute-start.13
  492.8 2.4 collective-permute-done.13
  496.7 2.9 collective-permute-done.14
  499.7 2.4 stack.32
  502.1 6.0 all-to-all-start.7
  508.1 93.6 %all-to-all-done.7 = bf16[16,512,256]{2,1,0:T(8,128)(2,1)} async-done(((bf16[16,512,256]{2,1,0:T(8,128)(2,1)}), bf16[16,512,256]{2,1,0:T(8,128)(2,1)}, u32[]{:S(2)}, u32[]{:S(2)}) %all-to-all-start.7) | async-done | bytes 4194336 | tf_op jit(solution)/shard_map/all_to_all | solution.py:10
  601.7 2.7 copy.46
  606.2 3.0 collective-permute-start.15
  611.9 1.6 collective-permute-done.16
  613.5 2.8 collective-permute-start.17
  616.3 1.9 collective-permute-done.17
  619.6 2.6 collective-permute-done.18
  622.3 3.0 collective-permute-start.19
  625.3 4.9 collective-permute-done.19
  631.1 196.8 %all_to_all.49 = bf16[16,1024,256]{2,1,0:T(8,128)(2,1)} all-to-all(bf16[16,1024,256]{2,1,0:T(8,128)(2,1)S(1)} %stack.33), channel_id=1, replica_groups=mesh['leaf'=16,'blk'=16] {'blk'}, dimensions={0} | all-to-all | bytes 16777216 | tf_op jit(solution)/shard_map/all_to_all | solution.py:10
  827.9 8.3 copy.50
  836.2 5.6 fusion.10
  (110 shorter events, 34.7 us)
Async XLA Ops:
  0.6 73.2 %copy-start = (bf16[320,5120]{1,0:T(8,128)(2,1)S(1)}, bf16[320,5120]{1,0:T(8,128)(2,1)}, u32[]{:S(2)}) copy-start(bf16[320,5120]{1,0:T(8,128)(2,1)} %param.8) | copy-start | bytes 9830404
  74.9 1.8 copy-start.5
  74.9 5.4 copy-start.7
  76.7 62.5 %all-to-all-start.1 = ((bf16[16,320,256]{2,1,0:T(8,128)(2,1)}), bf16[16,320,256]{2,1,0:T(8,128)(2,1)S(1)}, u32[]{:S(2)}, u32[]{:S(2)}) async-start(bf16[16,320,256]{2,1,0:T(8,128)(2,1)} %broadcast_in_dim.5), calls=%async_computation.1 | async-start | bytes 5242880 | tf_op jit(solution)/shard_map/all_to_all | solution.py:22
  80.3 65.3 %slice-start.2 = ((bf16[4,64,256]{2,1,0:T(8,128)(2,1)}), bf16[1,64,256]{2,1,0:T(8,128)(2,1)S(1)}, s32[]{:S(2)}) async-start(bf16[4,64,256]{2,1,0:T(8,128)(2,1)} %param.10), calls=%async_computation.11 | async-start | bytes 65536 | tf_op jit(solution)/shard_map/slice | solution.py:82
  141.7 3.9 collective-permute-start
  145.7 2.9 collective-permute-start.1
  186.7 2.9 collective-permute-start.2
  190.7 32.1 %all-to-all-start.3 = ((bf16[16,128,256]{2,1,0:T(8,128)(2,1)}), bf16[16,128,256]{2,1,0:T(8,128)(2,1)S(1)}, u32[]{:S(2)}, u32[]{:S(2)}) async-start(bf16[16,128,256]{2,1,0:T(8,128)(2,1)} %stack.26), calls=%async_computation.3 | async-start | bytes 2097152 | tf_op jit(solution)/shard_map/all_to_all | solution.py:10
  194.9 35.3 %copy-start.6 = (bf16[4,64,256]{2,1,0:T(8,128)(2,1)S(1)}, bf16[4,64,256]{2,1,0:T(8,128)(2,1)}, u32[]{:S(2)}) copy-start(bf16[4,64,256]{2,1,0:T(8,128)(2,1)} %param.10) | copy-start | bytes 393220
  225.0 5.2 collective-permute-start.3
  230.2 81.7 %copy-start.4 = (f32[3,64,256]{2,1,0:T(8,128)}, f32[3,64,256]{2,1,0:T(8,128)S(1)}, u32[]{:S(2)}) copy-start(f32[3,64,256]{2,1,0:T(8,128)S(1)} %copy_add_fusion.1) | copy-start | bytes 589828
  230.2 3.3 collective-permute-start.4
  233.5 4.7 collective-permute-start.5
  297.4 2.9 collective-permute-start.6
  300.3 5.3 collective-permute-start.7
  307.1 53.8 %all-to-all-start.5 = ((bf16[16,256,256]{2,1,0:T(8,128)(2,1)}), bf16[16,256,256]{2,1,0:T(8,128)(2,1)S(1)}, u32[]{:S(2)}, u32[]{:S(2)}) async-start(bf16[16,256,256]{2,1,0:T(8,128)(2,1)} %stack.29), calls=%async_computation.5 | async-start | bytes 4194304 | tf_op jit(solution)/shard_map/all_to_all | solution.py:10
  311.9 49.2 %slice-start.1 = ((f32[3,64,256]{2,1,0:T(8,128)}), f32[2,64,256]{2,1,0:T(8,128)S(1)}, s32[]{:S(2)}) async-start(f32[3,64,256]{2,1,0:T(8,128)} %copy-done.4), calls=%async_computation.10 | async-start | bytes 262144 | tf_op jit(solution)/shard_map/slice | solution.py:99
  363.4 4.3 collective-permute-start.8
  367.8 140.4 %copy-start.3 = (f32[3,64,256]{2,1,0:T(8,128)}, f32[3,64,256]{2,1,0:T(8,128)S(1)}, u32[]{:S(2)}) copy-start(f32[3,64,256]{2,1,0:T(8,128)S(1)} %copy_add_fusion) | copy-start | bytes 589828
  367.8 2.9 collective-permute-start.9
  370.7 4.7 collective-permute-start.10
  375.4 3.9 collective-permute-start.11
  487.1 2.9 collective-permute-start.12
  490.0 5.3 collective-permute-start.13
  495.3 4.3 collective-permute-start.14
  502.1 99.5 %all-to-all-start.7 = ((bf16[16,512,256]{2,1,0:T(8,128)(2,1)}), bf16[16,512,256]{2,1,0:T(8,128)(2,1)}, u32[]{:S(2)}, u32[]{:S(2)}) async-start(bf16[16,512,256]{2,1,0:T(8,128)(2,1)} %stack.32), calls=%async_computation.7 | async-start | bytes 8388608 | tf_op jit(solution)/shard_map/all_to_all | solution.py:10
  601.7 3.3 copy-start.2
  601.7 3.3 slice-start
  606.2 4.4 collective-permute-start.15
  610.6 2.9 collective-permute-start.16
  613.5 4.7 collective-permute-start.17
  618.2 4.0 collective-permute-start.18
  622.3 7.9 collective-permute-start.19
  836.2 6.3 copy-start.1
